TPU v7x, 32 devices: a whole 2x2x4 slice. The times are simulated.
32 devices in a mesh: blk: 8 (over z, x), grp: 4 (over y, core).
Axes of the slice: x: 2, y: 2, z: 4, core: 2. Of those that a mesh axis runs over, the one named last changes fastest.
Arguments:
- source_coords: float32 [3, 20480], P(None, ('blk', 'grp')), may hold values from 0 to 8, as said below
- source_values: float32 [3, 20480], P(None, ('blk', 'grp')), may hold values from -48 to 48
- target_coords: float32 [3, 16384], P(None, ('blk', 'grp')), may hold values from 0 to 8, as said below
- target_owner: int32 [16384], P(('blk', 'grp')), may hold values from 0 to 7, as said below
Outputs:
- weights: float32 [3, 20480], P(None, ('blk', 'grp'))
- poly: float32 [3, 4], replicated
- mapped: float32 [3, 16384], P(None, ('blk', 'grp'))
Inputs may be any that keep to these rules, and one draw needn't show every extreme that they name: `source_coords`: source vertex j has its first coordinate between j // 2560 and j // 2560 + 1, and the other two between 0 and 1. `target_coords`: target vertex t has its first coordinate between target_owner[t] and target_owner[t] + 1, and the other two between 0 and 1. target_owner[t] differs from t // 2048 by at most one.
All inputs are finite; a program needn't handle non-finite values.
Results may differ from a plain program's by a relative error of at most 0.0003.
Values sent between devices are 32-bit elements; how exact they have to be, the bound alone decides.
A program may use at most 64 MiB of HBM per device.

v0:
```python
import math
import jax
import jax.numpy as jnp
from jax import lax
from jax.sharding import PartitionSpec as P

ITERS = 3
REACH = 2
precise = lax.Precision.HIGHEST
thin_factor = 0.6
tiny = 1e-06


def from_behind(value, axis, steps):
    count = lax.axis_size(axis)
    initial, last = (max(0, -steps), min(count, count - steps))
    return lax.ppermute(value, axis, [(source, source + steps) for source in range(initial, last)])


def kernel_tile(rows, cols, stretch):
    along = rows[0][None, :] - cols[0][:, None]
    across = rows[1][None, :] - cols[1][:, None]
    upward = rows[2][None, :] - cols[2][:, None]
    return jnp.exp(-(thin_factor * along * along + stretch * (across * across + upward * upward)))


def basis(points, partitions, sources):
    ones = jnp.ones_like(points[0])
    stacked = jnp.stack(
        [ones, 2.0 * points[0] / partitions - 1.0, 2.0 * points[1] - 1.0, 2.0 * points[2] - 1.0]
    )
    return stacked / math.sqrt(sources)


def least_squares(hessenberg, beta):
    count = len(hessenberg)
    right_side = [beta] + [jnp.zeros_like(beta) for k in range(count)]
    upper = []
    cosines = []
    sines = []
    for k in range(count):
        column = list(hessenberg[k])
        for i in range(k):
            top = cosines[i] * column[i] + sines[i] * column[i + 1]
            lower = -sines[i] * column[i] + cosines[i] * column[i + 1]
            column[i] = top
            column[i + 1] = lower
        radius = jnp.sqrt(column[k] * column[k] + column[k + 1] * column[k + 1])
        cosine = column[k] / radius
        sine = column[k + 1] / radius
        column[k] = radius
        cosines.append(cosine)
        sines.append(sine)
        right_side[k + 1] = -sine * right_side[k]
        right_side[k] = cosine * right_side[k]
        upper.append(column[: k + 1])
    solved = [None] * count
    for k in reversed(range(count)):
        running = right_side[k]
        for j in range(k + 1, count):
            running = running - upper[j][k] * solved[j]
        solved[k] = running / upper[k][k]
    return solved


def near_slabs(block, reach):
    slab = lax.all_gather(block, "grp", axis=1, tiled=True)
    pieces = []
    for offset in range(-reach, reach + 1):
        if offset == 0:
            pieces.append(slab)
        else:
            pieces.append(from_behind(slab, "blk", -offset))
    return jnp.stack(pieces)


def apply_near(rows, near_coords, near_values, owners, first_slab, stretch, reach):
    labels = jnp.arange(near_coords.shape[0], dtype=jnp.int32) + first_slab

    def add_slab(running, item):
        cols, values, slab = item
        tile = kernel_tile(rows, cols, stretch)
        if owners is not None:
            tile = jnp.where((jnp.abs(owners - slab) <= reach)[None, :], tile, 0.0)
        return (
            running + jnp.dot(values, tile, precision=precise, preferred_element_type=jnp.float32),
            None,
        )

    start = jnp.zeros((near_values.shape[1], rows.shape[1]), jnp.float32)
    result, unused = lax.scan(add_slab, start, (near_coords, near_values, labels))
    return result


def shards(source_coords, source_values, target_coords, target_owner):
    reach = REACH
    own_rows = source_coords.shape[1]
    slab_len = own_rows * lax.axis_size("grp")
    partitions = lax.axis_size("blk")
    sources = slab_len * partitions
    stretch = 4.0 * slab_len
    here = lax.axis_index("blk")
    poly_src = basis(source_coords, partitions, sources)
    start_sq, start_moment = lax.psum(
        (
            jnp.sum(source_values * source_values, axis=1),
            jnp.dot(
                source_values, poly_src.T, precision=precise, preferred_element_type=jnp.float32
            ),
        ),
        ("blk", "grp"),
    )
    beta = jnp.sqrt(start_sq + tiny)
    heads = [source_values / beta[:, None]]
    tails = [jnp.zeros_like(start_moment)]
    moments = [start_moment / beta[:, None]]
    hessenberg = []
    for k in range(ITERS):
        both_near = near_slabs(jnp.concatenate([source_coords, heads[k]], axis=0), reach)
        cols = both_near[:, :3]
        values_near = both_near[:, 3:]
        image_head = apply_near(
            source_coords, cols, values_near, None, here - reach, stretch, reach
        ) + jnp.dot(tails[k], poly_src, precision=precise, preferred_element_type=jnp.float32)
        image_tail = moments[k]
        column = []
        local_dots = jnp.stack(
            [jnp.sum(heads[i] * image_head, axis=1) for i in range(k + 1)], axis=1
        )
        head_dots, image_sq, image_moment = lax.psum(
            (
                local_dots,
                jnp.sum(image_head * image_head, axis=1),
                jnp.dot(
                    image_head, poly_src.T, precision=precise, preferred_element_type=jnp.float32
                ),
            ),
            ("blk", "grp"),
        )
        full_sq = image_sq + jnp.sum(image_tail * image_tail, axis=1)
        rest_head = image_head
        rest_tail = image_tail
        rest_moment = image_moment
        for i in range(k + 1):
            factor = head_dots[:, i] + jnp.sum(tails[i] * image_tail, axis=1)
            full_sq = full_sq - factor * factor
            rest_head = rest_head - factor[:, None] * heads[i]
            rest_tail = rest_tail - factor[:, None] * tails[i]
            rest_moment = rest_moment - factor[:, None] * moments[i]
            column.append(factor)
        length = jnp.sqrt(full_sq + tiny)
        column.append(length)
        hessenberg.append(column)
        heads.append(rest_head / length[:, None])
        tails.append(rest_tail / length[:, None])
        moments.append(rest_moment / length[:, None])
    solved = least_squares(hessenberg, beta)
    weights = solved[0][:, None] * heads[0]
    poly = solved[0][:, None] * tails[0]
    for k in range(1, ITERS):
        weights = weights + solved[k][:, None] * heads[k]
        poly = poly + solved[k][:, None] * tails[k]
    joined_near = near_slabs(jnp.concatenate([source_coords, weights], axis=0), reach + 1)
    cols_far = joined_near[:, :3]
    weights_near = joined_near[:, 3:]
    poly_tgt = basis(target_coords, partitions, sources)
    mapped = apply_near(
        target_coords, cols_far, weights_near, target_owner, here - reach - 1, stretch, reach
    )
    mapped = mapped + jnp.dot(poly, poly_tgt, precision=precise, preferred_element_type=jnp.float32)
    return (weights, poly, mapped)


def solution(mesh):
    return jax.shard_map(
        shards,
        mesh=mesh,
        in_specs=(
            P(None, ("blk", "grp")),
            P(None, ("blk", "grp")),
            P(None, ("blk", "grp")),
            P(("blk", "grp")),
        ),
        out_specs=(P(None, ("blk", "grp")), P(), P(None, ("blk", "grp"))),
        check_vma=False,
    )
```

profile of v0, /device:TPU:6, one launch (start us, length us, event | category | flops | bytes accessed | tf_op | source)
XLA Modules:
  0.0 393.1 jit_solution(17570499681100357009)
XLA Ops:
  1.5 40.3 %psum.70 = f32[3]{0:T(128)S(1)} all-reduce(f32[3]{0:T(128)S(1)} %multiply_reduce_fusion.9), channel_id=1, replica_groups=mesh['blk'=8,'grp'=4] {'blk','grp'}, use_global_device_ids=true, to_apply=%region_1.0 | all-reduce | flops 3 | bytes 24 | tf_op jit(solution)/shard_map/psum | solution.py:104
  43.3 5.3 %all_gather.12 = f32[6,2560]{1,0:T(8,128)S(1)} all-gather(f32[6,640]{1,0:T(8,128)S(1)} %pad_maximum_fusion.3), channel_id=1, replica_groups=mesh['blk'=8,'grp'=4] {'grp'}, dimensions={1}, use_global_device_ids=true | all-gather | bytes 76800 | tf_op jit(solution)/shard_map/all_gather | solution.py:67
  64.5 29.7 %while.44 = (s32[]{:T(128)}, f32[3,640]{1,0:T(4,128)S(1)}, f32[5,3,2560]{2,1,0:T(4,128)S(1)}, f32[3,640]{1,0:T(4,128)S(1)}, f32[5,3,2560]{2,1,0:T(4,128)S(1)}, /*index=5*/s32[]{:T(128)}, s32[]{:T(128)}, s32[]{}, s32[]{}) while((s32[]{:T(128)}, f32[3,640]{1,0:T(4,128)S(1)}, f32[5,3,2560]{2,1,0:T(4,128)S(1)}, ...), condition=%wide.region_3.4_spmd.clone, body=%wide.region_2.0_spmd.clone.sunk | while | flops 77008640 | bytes 184975 | solution.py:91
  64.7 5.8 %fusion.163 = f32[3,640]{1,0:T(4,128)S(1)} fusion(f32[2560]{0:T(1024)S(1)} %get-tuple-element.469, f32[640]{0:T(1024)S(1)} %get-tuple-element.470, f32[2560]{0:T(1024)S(1)} %get-tuple-element.471, f32[640]{0:T(1024)S(1)} %get-tuple-element.472, f32[2560]{0:T(1024)S(1)} %get-tuple-element.473, f32[640]{0:T(1024)S(1)} %get-tuple-element.474, ...), kind=kOutput, calls=%fused_computation.20.clone.1 | convolution fusion | flops 77008640 | bytes 108037 | tf_op jit(solution)/shard_map/while/body/eval_jaxpr/dot_general | solution.py:86
  70.6 5.8 %fusion.163 = f32[3,640]{1,0:T(4,128)S(1)} fusion(f32[2560]{0:T(1024)S(1)} %get-tuple-element.469, f32[640]{0:T(1024)S(1)} %get-tuple-element.470, f32[2560]{0:T(1024)S(1)} %get-tuple-element.471, f32[640]{0:T(1024)S(1)} %get-tuple-element.472, f32[2560]{0:T(1024)S(1)} %get-tuple-element.473, f32[640]{0:T(1024)S(1)} %get-tuple-element.474, ...), kind=kOutput, calls=%fused_computation.20.clone.1 | convolution fusion | flops 77008640 | bytes 108037 | tf_op jit(solution)/shard_map/while/body/eval_jaxpr/dot_general | solution.py:86
  76.6 5.8 %fusion.163 = f32[3,640]{1,0:T(4,128)S(1)} fusion(f32[2560]{0:T(1024)S(1)} %get-tuple-element.469, f32[640]{0:T(1024)S(1)} %get-tuple-element.470, f32[2560]{0:T(1024)S(1)} %get-tuple-element.471, f32[640]{0:T(1024)S(1)} %get-tuple-element.472, f32[2560]{0:T(1024)S(1)} %get-tuple-element.473, f32[640]{0:T(1024)S(1)} %get-tuple-element.474, ...), kind=kOutput, calls=%fused_computation.20.clone.1 | convolution fusion | flops 77008640 | bytes 108037 | tf_op jit(solution)/shard_map/while/body/eval_jaxpr/dot_general | solution.py:86
  82.5 5.8 %fusion.163 = f32[3,640]{1,0:T(4,128)S(1)} fusion(f32[2560]{0:T(1024)S(1)} %get-tuple-element.469, f32[640]{0:T(1024)S(1)} %get-tuple-element.470, f32[2560]{0:T(1024)S(1)} %get-tuple-element.471, f32[640]{0:T(1024)S(1)} %get-tuple-element.472, f32[2560]{0:T(1024)S(1)} %get-tuple-element.473, f32[640]{0:T(1024)S(1)} %get-tuple-element.474, ...), kind=kOutput, calls=%fused_computation.20.clone.1 | convolution fusion | flops 77008640 | bytes 108037 | tf_op jit(solution)/shard_map/while/body/eval_jaxpr/dot_general | solution.py:86
  88.4 5.8 %fusion.163 = f32[3,640]{1,0:T(4,128)S(1)} fusion(f32[2560]{0:T(1024)S(1)} %get-tuple-element.469, f32[640]{0:T(1024)S(1)} %get-tuple-element.470, f32[2560]{0:T(1024)S(1)} %get-tuple-element.471, f32[640]{0:T(1024)S(1)} %get-tuple-element.472, f32[2560]{0:T(1024)S(1)} %get-tuple-element.473, f32[640]{0:T(1024)S(1)} %get-tuple-element.474, ...), kind=kOutput, calls=%fused_computation.20.clone.1 | convolution fusion | flops 77008640 | bytes 108037 | tf_op jit(solution)/shard_map/while/body/eval_jaxpr/dot_general | solution.py:86
  94.6 41.4 %all-reduce.2 = (f32[3]{0:T(128)S(1)}, f32[3,4]{1,0:T(4,128)S(1)}, f32[3,1]{0,1:T(1,128)S(1)}) all-reduce(f32[3]{0:T(128)S(1)} %get-tuple-element.232, f32[3,4]{1,0:T(4,128)S(1)} %convolution_bitcast_fusion, f32[3,1]{0,1:T(1,128)S(1)} %bitcast.208), channel_id=1, replica_groups=mesh['blk'=8,'grp'=4] {'blk','grp'}, use_global_device_ids=true, to_apply=%region_9.10 | all-reduce | flops 18 | bytes 144 | tf_op jit(solution)/shard_map/psum | solution.py:130
  136.3 5.3 %all_gather.13 = f32[6,2560]{1,0:T(8,128)S(1)} all-gather(f32[6,640]{1,0:T(8,128)S(1)} %pad_maximum_fusion.2), channel_id=1, replica_groups=mesh['blk'=8,'grp'=4] {'grp'}, dimensions={1}, use_global_device_ids=true | all-gather | bytes 76800 | tf_op jit(solution)/shard_map/all_gather | solution.py:67
  155.8 29.7 %while.45 = (s32[]{:T(128)}, f32[3,640]{1,0:T(4,128)S(1)}, f32[5,3,2560]{2,1,0:T(4,128)S(1)}, f32[3,640]{1,0:T(4,128)S(1)}, f32[5,3,2560]{2,1,0:T(4,128)S(1)}, /*index=5*/s32[]{:T(128)}, s32[]{:T(128)}, s32[]{}, s32[]{}) while((s32[]{:T(128)}, f32[3,640]{1,0:T(4,128)S(1)}, f32[5,3,2560]{2,1,0:T(4,128)S(1)}, ...), condition=%wide.region_12.13_spmd.clone, body=%wide.region_11.12_spmd.clone.sunk | while | flops 77008640 | bytes 184975 | solution.py:91
  156.0 5.8 %fusion.166 = f32[3,640]{1,0:T(4,128)S(1)} fusion(f32[2560]{0:T(1024)S(1)} %get-tuple-element.480, f32[640]{0:T(1024)S(1)} %get-tuple-element.481, f32[2560]{0:T(1024)S(1)} %get-tuple-element.482, f32[640]{0:T(1024)S(1)} %get-tuple-element.483, f32[2560]{0:T(1024)S(1)} %get-tuple-element.484, f32[640]{0:T(1024)S(1)} %get-tuple-element.485, ...), kind=kOutput, calls=%fused_computation.52.clone.1 | convolution fusion | flops 77008640 | bytes 108037 | tf_op jit(solution)/shard_map/while/body/eval_jaxpr/dot_general | solution.py:86
  161.9 5.8 %fusion.166 = f32[3,640]{1,0:T(4,128)S(1)} fusion(f32[2560]{0:T(1024)S(1)} %get-tuple-element.480, f32[640]{0:T(1024)S(1)} %get-tuple-element.481, f32[2560]{0:T(1024)S(1)} %get-tuple-element.482, f32[640]{0:T(1024)S(1)} %get-tuple-element.483, f32[2560]{0:T(1024)S(1)} %get-tuple-element.484, f32[640]{0:T(1024)S(1)} %get-tuple-element.485, ...), kind=kOutput, calls=%fused_computation.52.clone.1 | convolution fusion | flops 77008640 | bytes 108037 | tf_op jit(solution)/shard_map/while/body/eval_jaxpr/dot_general | solution.py:86
  167.8 5.8 %fusion.166 = f32[3,640]{1,0:T(4,128)S(1)} fusion(f32[2560]{0:T(1024)S(1)} %get-tuple-element.480, f32[640]{0:T(1024)S(1)} %get-tuple-element.481, f32[2560]{0:T(1024)S(1)} %get-tuple-element.482, f32[640]{0:T(1024)S(1)} %get-tuple-element.483, f32[2560]{0:T(1024)S(1)} %get-tuple-element.484, f32[640]{0:T(1024)S(1)} %get-tuple-element.485, ...), kind=kOutput, calls=%fused_computation.52.clone.1 | convolution fusion | flops 77008640 | bytes 108037 | tf_op jit(solution)/shard_map/while/body/eval_jaxpr/dot_general | solution.py:86
  173.8 5.8 %fusion.166 = f32[3,640]{1,0:T(4,128)S(1)} fusion(f32[2560]{0:T(1024)S(1)} %get-tuple-element.480, f32[640]{0:T(1024)S(1)} %get-tuple-element.481, f32[2560]{0:T(1024)S(1)} %get-tuple-element.482, f32[640]{0:T(1024)S(1)} %get-tuple-element.483, f32[2560]{0:T(1024)S(1)} %get-tuple-element.484, f32[640]{0:T(1024)S(1)} %get-tuple-element.485, ...), kind=kOutput, calls=%fused_computation.52.clone.1 | convolution fusion | flops 77008640 | bytes 108037 | tf_op jit(solution)/shard_map/while/body/eval_jaxpr/dot_general | solution.py:86
  179.7 5.8 %fusion.166 = f32[3,640]{1,0:T(4,128)S(1)} fusion(f32[2560]{0:T(1024)S(1)} %get-tuple-element.480, f32[640]{0:T(1024)S(1)} %get-tuple-element.481, f32[2560]{0:T(1024)S(1)} %get-tuple-element.482, f32[640]{0:T(1024)S(1)} %get-tuple-element.483, f32[2560]{0:T(1024)S(1)} %get-tuple-element.484, f32[640]{0:T(1024)S(1)} %get-tuple-element.485, ...), kind=kOutput, calls=%fused_computation.52.clone.1 | convolution fusion | flops 77008640 | bytes 108037 | tf_op jit(solution)/shard_map/while/body/eval_jaxpr/dot_general | solution.py:86
  185.9 40.5 %all-reduce.1 = (f32[3]{0:T(128)S(1)}, f32[3,4]{1,0:T(4,128)S(1)}, f32[3,2]{0,1:T(2,128)S(1)}) all-reduce(f32[3]{0:T(128)S(1)} %get-tuple-element.229, f32[3,4]{1,0:T(4,128)S(1)} %fusion.135, f32[3,2]{0,1:T(2,128)S(1)} %pad_maximum_fusion.5), channel_id=1, replica_groups=mesh['blk'=8,'grp'=4] {'blk','grp'}, use_global_device_ids=true, to_apply=%region_20.21 | all-reduce | flops 21 | bytes 168 | tf_op jit(solution)/shard_map/psum | solution.py:130
  226.7 5.3 %all_gather.14 = f32[6,2560]{1,0:T(8,128)S(1)} all-gather(f32[6,640]{1,0:T(8,128)S(1)} %pad_maximum_fusion.1), channel_id=1, replica_groups=mesh['blk'=8,'grp'=4] {'grp'}, dimensions={1}, use_global_device_ids=true | all-gather | bytes 76800 | tf_op jit(solution)/shard_map/all_gather | solution.py:67
  246.4 29.7 %while.46 = (s32[]{:T(128)}, f32[3,640]{1,0:T(4,128)S(1)}, f32[5,3,2560]{2,1,0:T(4,128)S(1)}, f32[3,640]{1,0:T(4,128)S(1)}, f32[5,3,2560]{2,1,0:T(4,128)S(1)}, /*index=5*/s32[]{:T(128)}, s32[]{:T(128)}, s32[]{}, s32[]{}) while((s32[]{:T(128)}, f32[3,640]{1,0:T(4,128)S(1)}, f32[5,3,2560]{2,1,0:T(4,128)S(1)}, ...), condition=%wide.region_23.24_spmd.clone, body=%wide.region_22.23_spmd.clone.sunk | while | flops 77008640 | bytes 184975 | solution.py:91
  246.5 5.8 %fusion.169 = f32[3,640]{1,0:T(4,128)S(1)} fusion(f32[2560]{0:T(1024)S(1)} %get-tuple-element.491, f32[640]{0:T(1024)S(1)} %get-tuple-element.492, f32[2560]{0:T(1024)S(1)} %get-tuple-element.493, f32[640]{0:T(1024)S(1)} %get-tuple-element.494, f32[2560]{0:T(1024)S(1)} %get-tuple-element.495, f32[640]{0:T(1024)S(1)} %get-tuple-element.496, ...), kind=kOutput, calls=%fused_computation.84.clone.1 | convolution fusion | flops 77008640 | bytes 108037 | tf_op jit(solution)/shard_map/while/body/eval_jaxpr/dot_general | solution.py:86
  252.5 5.8 %fusion.169 = f32[3,640]{1,0:T(4,128)S(1)} fusion(f32[2560]{0:T(1024)S(1)} %get-tuple-element.491, f32[640]{0:T(1024)S(1)} %get-tuple-element.492, f32[2560]{0:T(1024)S(1)} %get-tuple-element.493, f32[640]{0:T(1024)S(1)} %get-tuple-element.494, f32[2560]{0:T(1024)S(1)} %get-tuple-element.495, f32[640]{0:T(1024)S(1)} %get-tuple-element.496, ...), kind=kOutput, calls=%fused_computation.84.clone.1 | convolution fusion | flops 77008640 | bytes 108037 | tf_op jit(solution)/shard_map/while/body/eval_jaxpr/dot_general | solution.py:86
  258.4 5.8 %fusion.169 = f32[3,640]{1,0:T(4,128)S(1)} fusion(f32[2560]{0:T(1024)S(1)} %get-tuple-element.491, f32[640]{0:T(1024)S(1)} %get-tuple-element.492, f32[2560]{0:T(1024)S(1)} %get-tuple-element.493, f32[640]{0:T(1024)S(1)} %get-tuple-element.494, f32[2560]{0:T(1024)S(1)} %get-tuple-element.495, f32[640]{0:T(1024)S(1)} %get-tuple-element.496, ...), kind=kOutput, calls=%fused_computation.84.clone.1 | convolution fusion | flops 77008640 | bytes 108037 | tf_op jit(solution)/shard_map/while/body/eval_jaxpr/dot_general | solution.py:86
  264.3 5.8 %fusion.169 = f32[3,640]{1,0:T(4,128)S(1)} fusion(f32[2560]{0:T(1024)S(1)} %get-tuple-element.491, f32[640]{0:T(1024)S(1)} %get-tuple-element.492, f32[2560]{0:T(1024)S(1)} %get-tuple-element.493, f32[640]{0:T(1024)S(1)} %get-tuple-element.494, f32[2560]{0:T(1024)S(1)} %get-tuple-element.495, f32[640]{0:T(1024)S(1)} %get-tuple-element.496, ...), kind=kOutput, calls=%fused_computation.84.clone.1 | convolution fusion | flops 77008640 | bytes 108037 | tf_op jit(solution)/shard_map/while/body/eval_jaxpr/dot_general | solution.py:86
  270.3 5.8 %fusion.169 = f32[3,640]{1,0:T(4,128)S(1)} fusion(f32[2560]{0:T(1024)S(1)} %get-tuple-element.491, f32[640]{0:T(1024)S(1)} %get-tuple-element.492, f32[2560]{0:T(1024)S(1)} %get-tuple-element.493, f32[640]{0:T(1024)S(1)} %get-tuple-element.494, f32[2560]{0:T(1024)S(1)} %get-tuple-element.495, f32[640]{0:T(1024)S(1)} %get-tuple-element.496, ...), kind=kOutput, calls=%fused_computation.84.clone.1 | convolution fusion | flops 77008640 | bytes 108037 | tf_op jit(solution)/shard_map/while/body/eval_jaxpr/dot_general | solution.py:86
  276.5 41.9 %all-reduce = (f32[3]{0:T(128)S(1)}, f32[3,4]{1,0:T(4,128)S(1)}, f32[3,3]{0,1:T(4,128)S(1)}) all-reduce(f32[3]{0:T(128)S(1)} %get-tuple-element.225, f32[3,4]{1,0:T(4,128)S(1)} %fusion.134, f32[3,3]{0,1:T(4,128)S(1)} %pad_maximum_fusion.4), channel_id=1, replica_groups=mesh['blk'=8,'grp'=4] {'blk','grp'}, use_global_device_ids=true, to_apply=%region_33.34 | all-reduce | flops 24 | bytes 192 | tf_op jit(solution)/shard_map/psum | solution.py:130
  318.8 5.3 %all_gather.15 = f32[6,2560]{1,0:T(8,128)S(1)} all-gather(f32[6,640]{1,0:T(8,128)S(1)} %pad_maximum_fusion), channel_id=1, replica_groups=mesh['blk'=8,'grp'=4] {'grp'}, dimensions={1}, use_global_device_ids=true | all-gather | bytes 76800 | tf_op jit(solution)/shard_map/all_gather | solution.py:67
  342.9 5.3 %collective-permute-done.17 = f32[6,2560]{1,0:T(8,128)S(1)} collective-permute-done((f32[6,2560]{1,0:T(8,128)S(1)}, f32[6,2560]{1,0:T(8,128)S(1)}, u32[]{:S(2)}, u32[]{:S(2)}) %collective-permute-start.17) | collective-permute-done | bytes 61472 | tf_op jit(solution)/shard_map/ppermute | solution.py:17
  348.9 43.3 %while.47 = (s32[]{:T(128)}, f32[3,512]{1,0:T(4,128)S(1)}, f32[7,3,2560]{2,1,0:T(4,128)S(1)}, s32[7]{0:T(128)S(1)}, s32[512]{0:T(512)S(1)}, /*index=5*/f32[3,512...) while((s32[]{:T(128)}, f32[3,512]{1,0:T(4,128)S(1)}, ...), condition=%wide.region_36.37_spmd.clone, body=%wide.region_35.36_spmd.clone.sunk | while | flops 62919172 | bytes 175279 | solution.py:91
  350.3 4.8 %fusion.173 = f32[3,512]{1,0:T(4,128)S(1)} fusion(f32[2560]{0:T(1024)S(1)} %get-tuple-element.504, f32[512]{0:T(512)S(1)} %bitcast.203, f32[2560]{0:T(1024)S(1)} %get-tuple-element.506, f32[512]{0:T(512)S(1)} %bitcast.204, f32[2560]{0:T(1024)S(1)} %get-tuple-element.508, f32[512]{0:T(512)S(1)} %bitcast.202, ...), kind=kOutput, calls=%fused_computation.119.clone.1 | convolution fusion | flops 62917632 | bytes 98821 | tf_op jit(solution)/shard_map/while/body/eval_jaxpr/dot_general | solution.py:86
  362.7 4.8 %fusion.173 = f32[3,512]{1,0:T(4,128)S(1)} fusion(f32[2560]{0:T(1024)S(1)} %get-tuple-element.504, f32[512]{0:T(512)S(1)} %bitcast.203, f32[2560]{0:T(1024)S(1)} %get-tuple-element.506, f32[512]{0:T(512)S(1)} %bitcast.204, f32[2560]{0:T(1024)S(1)} %get-tuple-element.508, f32[512]{0:T(512)S(1)} %bitcast.202, ...), kind=kOutput, calls=%fused_computation.119.clone.1 | convolution fusion | flops 62917632 | bytes 98821 | tf_op jit(solution)/shard_map/while/body/eval_jaxpr/dot_general | solution.py:86
  381.3 4.8 %fusion.173 = f32[3,512]{1,0:T(4,128)S(1)} fusion(f32[2560]{0:T(1024)S(1)} %get-tuple-element.504, f32[512]{0:T(512)S(1)} %bitcast.203, f32[2560]{0:T(1024)S(1)} %get-tuple-element.506, f32[512]{0:T(512)S(1)} %bitcast.204, f32[2560]{0:T(1024)S(1)} %get-tuple-element.508, f32[512]{0:T(512)S(1)} %bitcast.202, ...), kind=kOutput, calls=%fused_computation.119.clone.1 | convolution fusion | flops 62917632 | bytes 98821 | tf_op jit(solution)/shard_map/while/body/eval_jaxpr/dot_general | solution.py:86
  387.5 4.8 %fusion.173 = f32[3,512]{1,0:T(4,128)S(1)} fusion(f32[2560]{0:T(1024)S(1)} %get-tuple-element.504, f32[512]{0:T(512)S(1)} %bitcast.203, f32[2560]{0:T(1024)S(1)} %get-tuple-element.506, f32[512]{0:T(512)S(1)} %bitcast.204, f32[2560]{0:T(1024)S(1)} %get-tuple-element.508, f32[512]{0:T(512)S(1)} %bitcast.202, ...), kind=kOutput, calls=%fused_computation.119.clone.1 | convolution fusion | flops 62917632 | bytes 98821 | tf_op jit(solution)/shard_map/while/body/eval_jaxpr/dot_general | solution.py:86
  (170 shorter events, 94.6 us)
Async XLA Ops:
  48.5 13.5 %collective-permute-start = (f32[6,2560]{1,0:T(8,128)S(1)}, f32[6,2560]{1,0:T(8,128)S(1)}, u32[]{:S(2)}, u32[]{:S(2)}) collective-permute-start(f32[6,2560]{1,0:T(8,128)S(1)} %all_gather.12), channel_id=1, source_target_pairs={{0,8},{4,12},{8,16},{12,20},{16,24},{20,28},{1,9},{5,13},{9,17},{1... | collective-permute-start | bytes 184328 | tf_op jit(solution)/shard_map/ppermute | solution.py:17
  52.0 10.1 %collective-permute-start.1 = (f32[6,2560]{1,0:T(8,128)S(1)}, f32[6,2560]{1,0:T(8,128)S(1)}, u32[]{:S(2)}, u32[]{:S(2)}) collective-permute-start(f32[6,2560]{1,0:T(8,128)S(1)} %all_gather.12), channel_id=1, source_target_pairs={{0,4},{4,8},{8,12},{12,16},{16,20},{20,24},{24,28},{1,5},{5,9},{9,... | collective-permute-start | bytes 184328 | tf_op jit(solution)/shard_map/ppermute | solution.py:17
  56.2 7.4 %collective-permute-start.2 = (f32[6,2560]{1,0:T(8,128)S(1)}, f32[6,2560]{1,0:T(8,128)S(1)}, u32[]{:S(2)}, u32[]{:S(2)}) collective-permute-start(f32[6,2560]{1,0:T(8,128)S(1)} %all_gather.12), channel_id=1, source_target_pairs={{4,0},{8,4},{12,8},{16,12},{20,16},{24,20},{28,24},{5,1},{9,5},{13... | collective-permute-start | bytes 184328 | tf_op jit(solution)/shard_map/ppermute | solution.py:17
  58.1 6.3 %collective-permute-start.3 = (f32[6,2560]{1,0:T(8,128)S(1)}, f32[6,2560]{1,0:T(8,128)S(1)}, u32[]{:S(2)}, u32[]{:S(2)}) collective-permute-start(f32[6,2560]{1,0:T(8,128)S(1)} %all_gather.12), channel_id=1, source_target_pairs={{8,0},{12,4},{16,8},{20,12},{24,16},{28,20},{9,1},{13,5},{17,9},{2... | collective-permute-start | bytes 184328 | tf_op jit(solution)/shard_map/ppermute | solution.py:17
  62.1 2.4 copy-start
  64.5 71.7 %copy-start.1 = (f32[3,640]{1,0:T(4,128)S(1)}, f32[3,640]{1,0:T(4,128)}, u32[]{:S(2)}) copy-start(f32[3,640]{1,0:T(4,128)} %param.13) | copy-start | bytes 23044
  141.6 9.5 %collective-permute-start.4 = (f32[6,2560]{1,0:T(8,128)S(1)}, f32[6,2560]{1,0:T(8,128)S(1)}, u32[]{:S(2)}, u32[]{:S(2)}) collective-permute-start(f32[6,2560]{1,0:T(8,128)S(1)} %all_gather.13), channel_id=1, source_target_pairs={{0,8},{4,12},{8,16},{12,20},{16,24},{20,28},{1,9},{5,13},{9,17},{1... | collective-permute-start | bytes 184328 | tf_op jit(solution)/shard_map/ppermute | solution.py:17
  143.5 7.6 %collective-permute-start.5 = (f32[6,2560]{1,0:T(8,128)S(1)}, f32[6,2560]{1,0:T(8,128)S(1)}, u32[]{:S(2)}, u32[]{:S(2)}) collective-permute-start(f32[6,2560]{1,0:T(8,128)S(1)} %all_gather.13), channel_id=1, source_target_pairs={{0,4},{4,8},{8,12},{12,16},{16,20},{20,24},{24,28},{1,5},{5,9},{9,... | collective-permute-start | bytes 184328 | tf_op jit(solution)/shard_map/ppermute | solution.py:17
  146.4 7.4 %collective-permute-start.6 = (f32[6,2560]{1,0:T(8,128)S(1)}, f32[6,2560]{1,0:T(8,128)S(1)}, u32[]{:S(2)}, u32[]{:S(2)}) collective-permute-start(f32[6,2560]{1,0:T(8,128)S(1)} %all_gather.13), channel_id=1, source_target_pairs={{4,0},{8,4},{12,8},{16,12},{20,16},{24,20},{28,24},{5,1},{9,5},{13... | collective-permute-start | bytes 184328 | tf_op jit(solution)/shard_map/ppermute | solution.py:17
  149.4 6.3 %collective-permute-start.7 = (f32[6,2560]{1,0:T(8,128)S(1)}, f32[6,2560]{1,0:T(8,128)S(1)}, u32[]{:S(2)}, u32[]{:S(2)}) collective-permute-start(f32[6,2560]{1,0:T(8,128)S(1)} %all_gather.13), channel_id=1, source_target_pairs={{8,0},{12,4},{16,8},{20,12},{24,16},{28,20},{9,1},{13,5},{17,9},{2... | collective-permute-start | bytes 184328 | tf_op jit(solution)/shard_map/ppermute | solution.py:17
  232.0 9.8 %collective-permute-start.8 = (f32[6,2560]{1,0:T(8,128)S(1)}, f32[6,2560]{1,0:T(8,128)S(1)}, u32[]{:S(2)}, u32[]{:S(2)}) collective-permute-start(f32[6,2560]{1,0:T(8,128)S(1)} %all_gather.14), channel_id=1, source_target_pairs={{0,8},{4,12},{8,16},{12,20},{16,24},{20,28},{1,9},{5,13},{9,17},{1... | collective-permute-start | bytes 184328 | tf_op jit(solution)/shard_map/ppermute | solution.py:17
  234.1 7.7 %collective-permute-start.9 = (f32[6,2560]{1,0:T(8,128)S(1)}, f32[6,2560]{1,0:T(8,128)S(1)}, u32[]{:S(2)}, u32[]{:S(2)}) collective-permute-start(f32[6,2560]{1,0:T(8,128)S(1)} %all_gather.14), channel_id=1, source_target_pairs={{0,4},{4,8},{8,12},{12,16},{16,20},{20,24},{24,28},{1,5},{5,9},{9,... | collective-permute-start | bytes 184328 | tf_op jit(solution)/shard_map/ppermute | solution.py:17
  237.7 7.4 %collective-permute-start.10 = (f32[6,2560]{1,0:T(8,128)S(1)}, f32[6,2560]{1,0:T(8,128)S(1)}, u32[]{:S(2)}, u32[]{:S(2)}) collective-permute-start(f32[6,2560]{1,0:T(8,128)S(1)} %all_gather.14), channel_id=1, source_target_pairs={{4,0},{8,4},{12,8},{16,12},{20,16},{24,20},{28,24},{5,1},{9,5},{13... | collective-permute-start | bytes 184328 | tf_op jit(solution)/shard_map/ppermute | solution.py:17
  240.0 6.3 %collective-permute-start.11 = (f32[6,2560]{1,0:T(8,128)S(1)}, f32[6,2560]{1,0:T(8,128)S(1)}, u32[]{:S(2)}, u32[]{:S(2)}) collective-permute-start(f32[6,2560]{1,0:T(8,128)S(1)} %all_gather.14), channel_id=1, source_target_pairs={{8,0},{12,4},{16,8},{20,12},{24,16},{28,20},{9,1},{13,5},{17,9},{2... | collective-permute-start | bytes 184328 | tf_op jit(solution)/shard_map/ppermute | solution.py:17
  318.8 29.5 %copy-start.4 = (f32[3,640]{1,0:T(4,128)}, f32[3,640]{1,0:T(4,128)S(1)}, u32[]{:S(2)}) copy-start(f32[3,640]{1,0:T(4,128)S(1)} %multiply_add_fusion) | copy-start | bytes 23044
  324.1 13.4 %collective-permute-start.12 = (f32[6,2560]{1,0:T(8,128)S(1)}, f32[6,2560]{1,0:T(8,128)S(1)}, u32[]{:S(2)}, u32[]{:S(2)}) collective-permute-start(f32[6,2560]{1,0:T(8,128)S(1)} %all_gather.15), channel_id=1, source_target_pairs={{0,12},{4,16},{8,20},{12,24},{16,28},{1,13},{5,17},{9,21},{13,25},... | collective-permute-start | bytes 184328 | tf_op jit(solution)/shard_map/ppermute | solution.py:17
  326.3 12.8 %collective-permute-start.13 = (f32[6,2560]{1,0:T(8,128)S(1)}, f32[6,2560]{1,0:T(8,128)S(1)}, u32[]{:S(2)}, u32[]{:S(2)}) collective-permute-start(f32[6,2560]{1,0:T(8,128)S(1)} %all_gather.15), channel_id=1, source_target_pairs={{0,8},{4,12},{8,16},{12,20},{16,24},{20,28},{1,9},{5,13},{9,17},{1... | collective-permute-start | bytes 184328 | tf_op jit(solution)/shard_map/ppermute | solution.py:17
  330.3 8.9 %collective-permute-start.14 = (f32[6,2560]{1,0:T(8,128)S(1)}, f32[6,2560]{1,0:T(8,128)S(1)}, u32[]{:S(2)}, u32[]{:S(2)}) collective-permute-start(f32[6,2560]{1,0:T(8,128)S(1)} %all_gather.15), channel_id=1, source_target_pairs={{0,4},{4,8},{8,12},{12,16},{16,20},{20,24},{24,28},{1,5},{5,9},{9,... | collective-permute-start | bytes 184328 | tf_op jit(solution)/shard_map/ppermute | solution.py:17
  334.1 7.6 %collective-permute-start.15 = (f32[6,2560]{1,0:T(8,128)S(1)}, f32[6,2560]{1,0:T(8,128)S(1)}, u32[]{:S(2)}, u32[]{:S(2)}) collective-permute-start(f32[6,2560]{1,0:T(8,128)S(1)} %all_gather.15), channel_id=1, source_target_pairs={{4,0},{8,4},{12,8},{16,12},{20,16},{24,20},{28,24},{5,1},{9,5},{13... | collective-permute-start | bytes 184328 | tf_op jit(solution)/shard_map/ppermute | solution.py:17
  336.1 6.8 %collective-permute-start.16 = (f32[6,2560]{1,0:T(8,128)S(1)}, f32[6,2560]{1,0:T(8,128)S(1)}, u32[]{:S(2)}, u32[]{:S(2)}) collective-permute-start(f32[6,2560]{1,0:T(8,128)S(1)} %all_gather.15), channel_id=1, source_target_pairs={{8,0},{12,4},{16,8},{20,12},{24,16},{28,20},{9,1},{13,5},{17,9},{2... | collective-permute-start | bytes 184328 | tf_op jit(solution)/shard_map/ppermute | solution.py:17
  337.5 54.8 %copy-start.5 = (f32[3,4]{1,0:T(4,128)}, f32[3,4]{1,0:T(4,128)S(1)}, u32[]{:S(2)}) copy-start(f32[3,4]{1,0:T(4,128)S(1)} %multiply_add_fusion.7) | copy-start | bytes 148
  337.5 10.7 %collective-permute-start.17 = (f32[6,2560]{1,0:T(8,128)S(1)}, f32[6,2560]{1,0:T(8,128)S(1)}, u32[]{:S(2)}, u32[]{:S(2)}) collective-permute-start(f32[6,2560]{1,0:T(8,128)S(1)} %all_gather.15), channel_id=1, source_target_pairs={{12,0},{16,4},{20,8},{24,12},{28,16},{13,1},{17,5},{21,9},{25,13},... | collective-permute-start | bytes 184328 | tf_op jit(solution)/shard_map/ppermute | solution.py:17
  348.2 0.7 copy-start.2
  348.3 0.7 copy-start.3
where the time goes:
time: 395 us; the launch traced here: 393 us
  blocking collectives  185 us (47%)
  matrix products  124 us (31%)
  starting transfers between devices  44.3 us (11%)
  waiting for transfers between devices  20.4 us (5%)
  other arithmetic  9.73 us (2%)
  local copies, waits for them, and re-layouts  7.71 us (2%)
    psum x3, blocking collectives, shards(): lax.psum((local_dots, jnp.sum(image_head * image_head, axis=1), jnp.dot(i...  124 us
    dot_general x22, matrix products, add_slab(): jnp.dot(values, tile, precision=precise, preferred_element_type=jnp.float32)  121 us
    ppermute x18, starting transfers between devices, from_behind(): lax.ppermute(value, axis, [(source, source + steps) for source in range(i...  44.3 us
    psum x1, blocking collectives, shards(): lax.psum((jnp.sum(source_values * source_values, axis=1), jnp.dot(source_...  40.3 us
    all_gather x4, blocking collectives, near_slabs(): slab = lax.all_gather(block, 'grp', axis=1, tiled=True)  21.1 us
    ppermute x18, waiting for transfers between devices, from_behind(): lax.ppermute(value, axis, [(source, source + steps) for source in range(i...  20.4 us
  transfers between devices with their start and end apart: 18, of which 9 were waited for; matrix products, arithmetic and copies ran while one was open for 1% of the time, Pallas kernels for 0%

commit v1 on v0

--- a/solution.py
+++ b/solution.py
@@ -128,14 +128,20 @@
             [jnp.sum(heads[i] * image_head, axis=1) for i in range(k + 1)], axis=1
         )
         head_dots, image_sq, image_moment = lax.psum(
-            (
-                local_dots,
-                jnp.sum(image_head * image_head, axis=1),
-                jnp.dot(
-                    image_head, poly_src.T, precision=precise, preferred_element_type=jnp.float32
+            lax.psum(
+                (
+                    local_dots,
+                    jnp.sum(image_head * image_head, axis=1),
+                    jnp.dot(
+                        image_head,
+                        poly_src.T,
+                        precision=precise,
+                        preferred_element_type=jnp.float32,
+                    ),
                 ),
+                "grp",
             ),
-            ("blk", "grp"),
+            "blk",
         )
         full_sq = image_sq + jnp.sum(image_tail * image_tail, axis=1)
         rest_head = image_head

time: 395 us -> 340 us (0.86)
  blocking collectives: 185 us -> 132 us
    psum x3, blocking collectives: 124 us -> 17.2 us  [shards(): lax.psum((local_dots, jnp.sum(image_head * image_head, axis=1), jnp.dot(i...]
    psum x0 -> x3, blocking collectives: none -> 53.7 us  [shards(): lax.psum(lax.psum((local_dots, jnp.sum(image_head * image_head, axis=1),...]
where the time goes in v1:
time: 340 us; the launch traced here: 339 us
  blocking collectives  132 us (39%)
  matrix products  124 us (36%)
  starting transfers between devices  41.2 us (12%)
  waiting for transfers between devices  22 us (6%)
  other arithmetic  9.76 us (3%)
  local copies, waits for them, and re-layouts  7.71 us (2%)
    dot_general x22, matrix products, add_slab(): jnp.dot(values, tile, precision=precise, preferred_element_type=jnp.float32)  121 us
    psum x3, blocking collectives, shards(): lax.psum(lax.psum((local_dots, jnp.sum(image_head * image_head, axis=1),...  53.7 us
    ppermute x18, starting transfers between devices, from_behind(): lax.ppermute(value, axis, [(source, source + steps) for source in range(i...  41.2 us
    psum x1, blocking collectives, shards(): lax.psum((jnp.sum(source_values * source_values, axis=1), jnp.dot(source_...  40.3 us
    ppermute x18, waiting for transfers between devices, from_behind(): lax.ppermute(value, axis, [(source, source + steps) for source in range(i...  22 us
    all_gather x4, blocking collectives, near_slabs(): slab = lax.all_gather(block, 'grp', axis=1, tiled=True)  21.1 us
    psum x3, blocking collectives, shards(): lax.psum((local_dots, jnp.sum(image_head * image_head, axis=1), jnp.dot(i...  17.2 us
  transfers between devices with their start and end apart: 18, of which 9 were waited for; matrix products, arithmetic and copies ran while one was open for 1% of the time, Pallas kernels for 0%

profile of v1, /device:TPU:6, one launch (start us, length us, event | category | flops | bytes accessed | tf_op | source)
XLA Modules:
  0.0 338.7 jit_solution(5934589819539855259)
XLA Ops:
  3.2 40.3 %all-reduce = (f32[3]{0:T(128)S(1)}, f32[3,4]{1,0:T(4,128)S(1)}) all-reduce(f32[3]{0:T(128)S(1)} %multiply_reduce_fusion.9, f32[3,4]{1,0:T(4,128)S(1)} %convolution_bitcast_fusion), channel_id=1, replica_groups=mesh['blk'=8,'grp'=4] {'blk','grp'}, use_global_device_ids=true, to_apply=%region_1.0 | all-reduce | flops 15 | bytes 120 | tf_op jit(solution)/shard_map/psum | solution.py:104
  45.1 5.3 %all_gather.12 = f32[6,2560]{1,0:T(8,128)S(1)} all-gather(f32[6,640]{1,0:T(8,128)S(1)} %pad_maximum_fusion.3), channel_id=1, replica_groups=mesh['blk'=8,'grp'=4] {'grp'}, dimensions={1}, use_global_device_ids=true | all-gather | bytes 76800 | tf_op jit(solution)/shard_map/all_gather | solution.py:67
  66.3 29.7 %while.44 = (s32[]{:T(128)}, f32[3,640]{1,0:T(4,128)S(1)}, f32[5,3,2560]{2,1,0:T(4,128)S(1)}, f32[3,640]{1,0:T(4,128)S(1)}, f32[5,3,2560]{2,1,0:T(4,128)S(1)}, /*index=5*/s32[]{:T(128)}, s32[]{:T(128)}, s32[]{}, s32[]{}) while((s32[]{:T(128)}, f32[3,640]{1,0:T(4,128)S(1)}, f32[5,3,2560]{2,1,0:T(4,128)S(1)}, ...), condition=%wide.region_3.4_spmd.clone, body=%wide.region_2.0_spmd.clone.sunk | while | flops 77008640 | bytes 184975 | solution.py:91
  66.5 5.8 %fusion.163 = f32[3,640]{1,0:T(4,128)S(1)} fusion(f32[2560]{0:T(1024)S(1)} %get-tuple-element.478, f32[640]{0:T(1024)S(1)} %get-tuple-element.479, f32[2560]{0:T(1024)S(1)} %get-tuple-element.480, f32[640]{0:T(1024)S(1)} %get-tuple-element.481, f32[2560]{0:T(1024)S(1)} %get-tuple-element.482, f32[640]{0:T(1024)S(1)} %get-tuple-element.483, ...), kind=kOutput, calls=%fused_computation.20.clone.1 | convolution fusion | flops 77008640 | bytes 108037 | tf_op jit(solution)/shard_map/while/body/eval_jaxpr/dot_general | solution.py:86
  72.4 5.8 %fusion.163 = f32[3,640]{1,0:T(4,128)S(1)} fusion(f32[2560]{0:T(1024)S(1)} %get-tuple-element.478, f32[640]{0:T(1024)S(1)} %get-tuple-element.479, f32[2560]{0:T(1024)S(1)} %get-tuple-element.480, f32[640]{0:T(1024)S(1)} %get-tuple-element.481, f32[2560]{0:T(1024)S(1)} %get-tuple-element.482, f32[640]{0:T(1024)S(1)} %get-tuple-element.483, ...), kind=kOutput, calls=%fused_computation.20.clone.1 | convolution fusion | flops 77008640 | bytes 108037 | tf_op jit(solution)/shard_map/while/body/eval_jaxpr/dot_general | solution.py:86
  78.4 5.8 %fusion.163 = f32[3,640]{1,0:T(4,128)S(1)} fusion(f32[2560]{0:T(1024)S(1)} %get-tuple-element.478, f32[640]{0:T(1024)S(1)} %get-tuple-element.479, f32[2560]{0:T(1024)S(1)} %get-tuple-element.480, f32[640]{0:T(1024)S(1)} %get-tuple-element.481, f32[2560]{0:T(1024)S(1)} %get-tuple-element.482, f32[640]{0:T(1024)S(1)} %get-tuple-element.483, ...), kind=kOutput, calls=%fused_computation.20.clone.1 | convolution fusion | flops 77008640 | bytes 108037 | tf_op jit(solution)/shard_map/while/body/eval_jaxpr/dot_general | solution.py:86
  84.3 5.8 %fusion.163 = f32[3,640]{1,0:T(4,128)S(1)} fusion(f32[2560]{0:T(1024)S(1)} %get-tuple-element.478, f32[640]{0:T(1024)S(1)} %get-tuple-element.479, f32[2560]{0:T(1024)S(1)} %get-tuple-element.480, f32[640]{0:T(1024)S(1)} %get-tuple-element.481, f32[2560]{0:T(1024)S(1)} %get-tuple-element.482, f32[640]{0:T(1024)S(1)} %get-tuple-element.483, ...), kind=kOutput, calls=%fused_computation.20.clone.1 | convolution fusion | flops 77008640 | bytes 108037 | tf_op jit(solution)/shard_map/while/body/eval_jaxpr/dot_general | solution.py:86
  90.2 5.8 %fusion.163 = f32[3,640]{1,0:T(4,128)S(1)} fusion(f32[2560]{0:T(1024)S(1)} %get-tuple-element.478, f32[640]{0:T(1024)S(1)} %get-tuple-element.479, f32[2560]{0:T(1024)S(1)} %get-tuple-element.480, f32[640]{0:T(1024)S(1)} %get-tuple-element.481, f32[2560]{0:T(1024)S(1)} %get-tuple-element.482, f32[640]{0:T(1024)S(1)} %get-tuple-element.483, ...), kind=kOutput, calls=%fused_computation.20.clone.1 | convolution fusion | flops 77008640 | bytes 108037 | tf_op jit(solution)/shard_map/while/body/eval_jaxpr/dot_general | solution.py:86
  96.4 5.7 %all-reduce.6 = (f32[3]{0:T(128)S(1)}, f32[3,1]{0,1:T(1,128)S(1)}) all-reduce(f32[3]{0:T(128)S(1)} %get-tuple-element.232, f32[3,1]{0,1:T(1,128)S(1)} %bitcast.210), channel_id=1, replica_groups=mesh['blk'=8,'grp'=4] {'grp'}, use_global_device_ids=true, to_apply=%region_10.11 | all-reduce | flops 6 | bytes 48 | tf_op jit(solution)/shard_map/psum | solution.py:131
  102.0 18.7 %all-reduce.3 = (f32[3]{0:T(128)S(1)}, f32[3,1]{0,1:T(1,128)S(1)}) all-reduce(f32[3]{0:T(128)S(1)} %get-tuple-element.302, f32[3,1]{0,1:T(1,128)S(1)} %get-tuple-element.303), channel_id=1, replica_groups=mesh['blk'=8,'grp'=4] {'blk'}, use_global_device_ids=true, to_apply=%region_11.12 | all-reduce | flops 6 | bytes 48 | tf_op jit(solution)/shard_map/psum | solution.py:130
  120.8 5.3 %all_gather.13 = f32[6,2560]{1,0:T(8,128)S(1)} all-gather(f32[6,640]{1,0:T(8,128)S(1)} %pad_maximum_fusion.2), channel_id=1, replica_groups=mesh['blk'=8,'grp'=4] {'grp'}, dimensions={1}, use_global_device_ids=true | all-gather | bytes 76800 | tf_op jit(solution)/shard_map/all_gather | solution.py:67
  139.7 29.7 %while.45 = (s32[]{:T(128)}, f32[3,640]{1,0:T(4,128)S(1)}, f32[5,3,2560]{2,1,0:T(4,128)S(1)}, f32[3,640]{1,0:T(4,128)S(1)}, f32[5,3,2560]{2,1,0:T(4,128)S(1)}, /*index=5*/s32[]{:T(128)}, s32[]{:T(128)}, s32[]{}, s32[]{}) while((s32[]{:T(128)}, f32[3,640]{1,0:T(4,128)S(1)}, f32[5,3,2560]{2,1,0:T(4,128)S(1)}, ...), condition=%wide.region_14.15_spmd.clone, body=%wide.region_13.14_spmd.clone.sunk | while | flops 77008640 | bytes 184975 | solution.py:91
  139.8 5.8 %fusion.166 = f32[3,640]{1,0:T(4,128)S(1)} fusion(f32[2560]{0:T(1024)S(1)} %get-tuple-element.489, f32[640]{0:T(1024)S(1)} %get-tuple-element.490, f32[2560]{0:T(1024)S(1)} %get-tuple-element.491, f32[640]{0:T(1024)S(1)} %get-tuple-element.492, f32[2560]{0:T(1024)S(1)} %get-tuple-element.493, f32[640]{0:T(1024)S(1)} %get-tuple-element.494, ...), kind=kOutput, calls=%fused_computation.52.clone.1 | convolution fusion | flops 77008640 | bytes 108037 | tf_op jit(solution)/shard_map/while/body/eval_jaxpr/dot_general | solution.py:86
  145.8 5.8 %fusion.166 = f32[3,640]{1,0:T(4,128)S(1)} fusion(f32[2560]{0:T(1024)S(1)} %get-tuple-element.489, f32[640]{0:T(1024)S(1)} %get-tuple-element.490, f32[2560]{0:T(1024)S(1)} %get-tuple-element.491, f32[640]{0:T(1024)S(1)} %get-tuple-element.492, f32[2560]{0:T(1024)S(1)} %get-tuple-element.493, f32[640]{0:T(1024)S(1)} %get-tuple-element.494, ...), kind=kOutput, calls=%fused_computation.52.clone.1 | convolution fusion | flops 77008640 | bytes 108037 | tf_op jit(solution)/shard_map/while/body/eval_jaxpr/dot_general | solution.py:86
  151.7 5.8 %fusion.166 = f32[3,640]{1,0:T(4,128)S(1)} fusion(f32[2560]{0:T(1024)S(1)} %get-tuple-element.489, f32[640]{0:T(1024)S(1)} %get-tuple-element.490, f32[2560]{0:T(1024)S(1)} %get-tuple-element.491, f32[640]{0:T(1024)S(1)} %get-tuple-element.492, f32[2560]{0:T(1024)S(1)} %get-tuple-element.493, f32[640]{0:T(1024)S(1)} %get-tuple-element.494, ...), kind=kOutput, calls=%fused_computation.52.clone.1 | convolution fusion | flops 77008640 | bytes 108037 | tf_op jit(solution)/shard_map/while/body/eval_jaxpr/dot_general | solution.py:86
  157.6 5.8 %fusion.166 = f32[3,640]{1,0:T(4,128)S(1)} fusion(f32[2560]{0:T(1024)S(1)} %get-tuple-element.489, f32[640]{0:T(1024)S(1)} %get-tuple-element.490, f32[2560]{0:T(1024)S(1)} %get-tuple-element.491, f32[640]{0:T(1024)S(1)} %get-tuple-element.492, f32[2560]{0:T(1024)S(1)} %get-tuple-element.493, f32[640]{0:T(1024)S(1)} %get-tuple-element.494, ...), kind=kOutput, calls=%fused_computation.52.clone.1 | convolution fusion | flops 77008640 | bytes 108037 | tf_op jit(solution)/shard_map/while/body/eval_jaxpr/dot_general | solution.py:86
  163.6 5.8 %fusion.166 = f32[3,640]{1,0:T(4,128)S(1)} fusion(f32[2560]{0:T(1024)S(1)} %get-tuple-element.489, f32[640]{0:T(1024)S(1)} %get-tuple-element.490, f32[2560]{0:T(1024)S(1)} %get-tuple-element.491, f32[640]{0:T(1024)S(1)} %get-tuple-element.492, f32[2560]{0:T(1024)S(1)} %get-tuple-element.493, f32[640]{0:T(1024)S(1)} %get-tuple-element.494, ...), kind=kOutput, calls=%fused_computation.52.clone.1 | convolution fusion | flops 77008640 | bytes 108037 | tf_op jit(solution)/shard_map/while/body/eval_jaxpr/dot_general | solution.py:86
  169.8 5.8 %all-reduce.5 = (f32[3]{0:T(128)S(1)}, f32[3,4]{1,0:T(4,128)S(1)}, f32[3,2]{0,1:T(2,128)S(1)}) all-reduce(f32[3]{0:T(128)S(1)} %get-tuple-element.229, f32[3,4]{1,0:T(4,128)S(1)} %fusion.135, f32[3,2]{0,1:T(2,128)S(1)} %pad_maximum_fusion.5), channel_id=1, replica_groups=mesh['blk'=8,'grp'=4] {'grp'}, use_global_device_ids=true, to_apply=%region_24.25 | all-reduce | flops 21 | bytes 168 | tf_op jit(solution)/shard_map/psum | solution.py:131
  175.5 16.7 %all-reduce.2 = (f32[3]{0:T(128)S(1)}, f32[3,4]{1,0:T(4,128)S(1)}, f32[3,2]{0,1:T(2,128)S(1)}) all-reduce(f32[3]{0:T(128)S(1)} %get-tuple-element.299, f32[3,4]{1,0:T(4,128)S(1)} %get-tuple-element.300, f32[3,2]{0,1:T(2,128)S(1)} %get-tuple-element.301), channel_id=1, replica_groups=mesh['blk'=8,'grp'=4] {'blk'}, use_global_device_ids=true, to_apply=%region_25.26 | all-reduce | flops 21 | bytes 168 | tf_op jit(solution)/shard_map/psum | solution.py:130
  192.6 5.3 %all_gather.14 = f32[6,2560]{1,0:T(8,128)S(1)} all-gather(f32[6,640]{1,0:T(8,128)S(1)} %pad_maximum_fusion.1), channel_id=1, replica_groups=mesh['blk'=8,'grp'=4] {'grp'}, dimensions={1}, use_global_device_ids=true | all-gather | bytes 76800 | tf_op jit(solution)/shard_map/all_gather | solution.py:67
  211.5 29.7 %while.46 = (s32[]{:T(128)}, f32[3,640]{1,0:T(4,128)S(1)}, f32[5,3,2560]{2,1,0:T(4,128)S(1)}, f32[3,640]{1,0:T(4,128)S(1)}, f32[5,3,2560]{2,1,0:T(4,128)S(1)}, /*index=5*/s32[]{:T(128)}, s32[]{:T(128)}, s32[]{}, s32[]{}) while((s32[]{:T(128)}, f32[3,640]{1,0:T(4,128)S(1)}, f32[5,3,2560]{2,1,0:T(4,128)S(1)}, ...), condition=%wide.region_28.29_spmd.clone, body=%wide.region_27.28_spmd.clone.sunk | while | flops 77008640 | bytes 184975 | solution.py:91
  211.7 5.8 %fusion.169 = f32[3,640]{1,0:T(4,128)S(1)} fusion(f32[2560]{0:T(1024)S(1)} %get-tuple-element.500, f32[640]{0:T(1024)S(1)} %get-tuple-element.501, f32[2560]{0:T(1024)S(1)} %get-tuple-element.502, f32[640]{0:T(1024)S(1)} %get-tuple-element.503, f32[2560]{0:T(1024)S(1)} %get-tuple-element.504, f32[640]{0:T(1024)S(1)} %get-tuple-element.505, ...), kind=kOutput, calls=%fused_computation.84.clone.1 | convolution fusion | flops 77008640 | bytes 108037 | tf_op jit(solution)/shard_map/while/body/eval_jaxpr/dot_general | solution.py:86
  217.6 5.8 %fusion.169 = f32[3,640]{1,0:T(4,128)S(1)} fusion(f32[2560]{0:T(1024)S(1)} %get-tuple-element.500, f32[640]{0:T(1024)S(1)} %get-tuple-element.501, f32[2560]{0:T(1024)S(1)} %get-tuple-element.502, f32[640]{0:T(1024)S(1)} %get-tuple-element.503, f32[2560]{0:T(1024)S(1)} %get-tuple-element.504, f32[640]{0:T(1024)S(1)} %get-tuple-element.505, ...), kind=kOutput, calls=%fused_computation.84.clone.1 | convolution fusion | flops 77008640 | bytes 108037 | tf_op jit(solution)/shard_map/while/body/eval_jaxpr/dot_general | solution.py:86
  223.5 5.8 %fusion.169 = f32[3,640]{1,0:T(4,128)S(1)} fusion(f32[2560]{0:T(1024)S(1)} %get-tuple-element.500, f32[640]{0:T(1024)S(1)} %get-tuple-element.501, f32[2560]{0:T(1024)S(1)} %get-tuple-element.502, f32[640]{0:T(1024)S(1)} %get-tuple-element.503, f32[2560]{0:T(1024)S(1)} %get-tuple-element.504, f32[640]{0:T(1024)S(1)} %get-tuple-element.505, ...), kind=kOutput, calls=%fused_computation.84.clone.1 | convolution fusion | flops 77008640 | bytes 108037 | tf_op jit(solution)/shard_map/while/body/eval_jaxpr/dot_general | solution.py:86
  229.5 5.8 %fusion.169 = f32[3,640]{1,0:T(4,128)S(1)} fusion(f32[2560]{0:T(1024)S(1)} %get-tuple-element.500, f32[640]{0:T(1024)S(1)} %get-tuple-element.501, f32[2560]{0:T(1024)S(1)} %get-tuple-element.502, f32[640]{0:T(1024)S(1)} %get-tuple-element.503, f32[2560]{0:T(1024)S(1)} %get-tuple-element.504, f32[640]{0:T(1024)S(1)} %get-tuple-element.505, ...), kind=kOutput, calls=%fused_computation.84.clone.1 | convolution fusion | flops 77008640 | bytes 108037 | tf_op jit(solution)/shard_map/while/body/eval_jaxpr/dot_general | solution.py:86
  235.4 5.8 %fusion.169 = f32[3,640]{1,0:T(4,128)S(1)} fusion(f32[2560]{0:T(1024)S(1)} %get-tuple-element.500, f32[640]{0:T(1024)S(1)} %get-tuple-element.501, f32[2560]{0:T(1024)S(1)} %get-tuple-element.502, f32[640]{0:T(1024)S(1)} %get-tuple-element.503, f32[2560]{0:T(1024)S(1)} %get-tuple-element.504, f32[640]{0:T(1024)S(1)} %get-tuple-element.505, ...), kind=kOutput, calls=%fused_computation.84.clone.1 | convolution fusion | flops 77008640 | bytes 108037 | tf_op jit(solution)/shard_map/while/body/eval_jaxpr/dot_general | solution.py:86
  241.6 5.8 %all-reduce.4 = (f32[3]{0:T(128)S(1)}, f32[3,4]{1,0:T(4,128)S(1)}, f32[3,3]{0,1:T(4,128)S(1)}) all-reduce(f32[3]{0:T(128)S(1)} %get-tuple-element.225, f32[3,4]{1,0:T(4,128)S(1)} %fusion.134, f32[3,3]{0,1:T(4,128)S(1)} %pad_maximum_fusion.4), channel_id=1, replica_groups=mesh['blk'=8,'grp'=4] {'grp'}, use_global_device_ids=true, to_apply=%region_40.41 | all-reduce | flops 24 | bytes 192 | tf_op jit(solution)/shard_map/psum | solution.py:131
  247.4 18.4 %all-reduce.1 = (f32[3]{0:T(128)S(1)}, f32[3,4]{1,0:T(4,128)S(1)}, f32[3,3]{0,1:T(4,128)S(1)}) all-reduce(f32[3]{0:T(128)S(1)} %get-tuple-element.296, f32[3,4]{1,0:T(4,128)S(1)} %get-tuple-element.297, f32[3,3]{0,1:T(4,128)S(1)} %get-tuple-element.298), channel_id=1, replica_groups=mesh['blk'=8,'grp'=4] {'blk'}, use_global_device_ids=true, to_apply=%region_41.42 | all-reduce | flops 24 | bytes 192 | tf_op jit(solution)/shard_map/psum | solution.py:130
  266.1 5.3 %all_gather.15 = f32[6,2560]{1,0:T(8,128)S(1)} all-gather(f32[6,640]{1,0:T(8,128)S(1)} %pad_maximum_fusion), channel_id=1, replica_groups=mesh['blk'=8,'grp'=4] {'grp'}, dimensions={1}, use_global_device_ids=true | all-gather | bytes 76800 | tf_op jit(solution)/shard_map/all_gather | solution.py:67
  288.4 5.5 %collective-permute-done.17 = f32[6,2560]{1,0:T(8,128)S(1)} collective-permute-done((f32[6,2560]{1,0:T(8,128)S(1)}, f32[6,2560]{1,0:T(8,128)S(1)}, u32[]{:S(2)}, u32[]{:S(2)}) %collective-permute-start.17) | collective-permute-done | bytes 61472 | tf_op jit(solution)/shard_map/ppermute | solution.py:17
  294.6 43.3 %while.47 = (s32[]{:T(128)}, f32[3,512]{1,0:T(4,128)S(1)}, f32[7,3,2560]{2,1,0:T(4,128)S(1)}, s32[7]{0:T(128)S(1)}, s32[512]{0:T(512)S(1)}, /*index=5*/f32[3,512...) while((s32[]{:T(128)}, f32[3,512]{1,0:T(4,128)S(1)}, ...), condition=%wide.region_44.45_spmd.clone, body=%wide.region_43.44_spmd.clone.sunk | while | flops 62919172 | bytes 175279 | solution.py:91
  302.1 4.8 %fusion.173 = f32[3,512]{1,0:T(4,128)S(1)} fusion(f32[2560]{0:T(1024)S(1)} %get-tuple-element.513, f32[512]{0:T(512)S(1)} %bitcast.203, f32[2560]{0:T(1024)S(1)} %get-tuple-element.515, f32[512]{0:T(512)S(1)} %bitcast.204, f32[2560]{0:T(1024)S(1)} %get-tuple-element.517, f32[512]{0:T(512)S(1)} %bitcast.202, ...), kind=kOutput, calls=%fused_computation.119.clone.1 | convolution fusion | flops 62917632 | bytes 98821 | tf_op jit(solution)/shard_map/while/body/eval_jaxpr/dot_general | solution.py:86
  (173 shorter events, 107.4 us)
Async XLA Ops:
  50.3 11.9 %collective-permute-start = (f32[6,2560]{1,0:T(8,128)S(1)}, f32[6,2560]{1,0:T(8,128)S(1)}, u32[]{:S(2)}, u32[]{:S(2)}) collective-permute-start(f32[6,2560]{1,0:T(8,128)S(1)} %all_gather.12), channel_id=1, source_target_pairs={{0,8},{4,12},{8,16},{12,20},{16,24},{20,28},{1,9},{5,13},{9,17},{1... | collective-permute-start | bytes 184328 | tf_op jit(solution)/shard_map/ppermute | solution.py:17
  53.7 8.5 %collective-permute-start.1 = (f32[6,2560]{1,0:T(8,128)S(1)}, f32[6,2560]{1,0:T(8,128)S(1)}, u32[]{:S(2)}, u32[]{:S(2)}) collective-permute-start(f32[6,2560]{1,0:T(8,128)S(1)} %all_gather.12), channel_id=1, source_target_pairs={{0,4},{4,8},{8,12},{12,16},{16,20},{20,24},{24,28},{1,5},{5,9},{9,... | collective-permute-start | bytes 184328 | tf_op jit(solution)/shard_map/ppermute | solution.py:17
  58.0 7.4 %collective-permute-start.2 = (f32[6,2560]{1,0:T(8,128)S(1)}, f32[6,2560]{1,0:T(8,128)S(1)}, u32[]{:S(2)}, u32[]{:S(2)}) collective-permute-start(f32[6,2560]{1,0:T(8,128)S(1)} %all_gather.12), channel_id=1, source_target_pairs={{4,0},{8,4},{12,8},{16,12},{20,16},{24,20},{28,24},{5,1},{9,5},{13... | collective-permute-start | bytes 184328 | tf_op jit(solution)/shard_map/ppermute | solution.py:17
  59.9 6.3 %collective-permute-start.3 = (f32[6,2560]{1,0:T(8,128)S(1)}, f32[6,2560]{1,0:T(8,128)S(1)}, u32[]{:S(2)}, u32[]{:S(2)}) collective-permute-start(f32[6,2560]{1,0:T(8,128)S(1)} %all_gather.12), channel_id=1, source_target_pairs={{8,0},{12,4},{16,8},{20,12},{24,16},{28,20},{9,1},{13,5},{17,9},{2... | collective-permute-start | bytes 184328 | tf_op jit(solution)/shard_map/ppermute | solution.py:17
  62.3 4.0 %copy-start = (f32[3,640]{1,0:T(4,128)S(1)}, f32[3,640]{1,0:T(4,128)}, u32[]{:S(2)}) copy-start(f32[3,640]{1,0:T(4,128)} %param.12) | copy-start | bytes 23044
  66.3 54.4 %copy-start.1 = (f32[3,640]{1,0:T(4,128)S(1)}, f32[3,640]{1,0:T(4,128)}, u32[]{:S(2)}) copy-start(f32[3,640]{1,0:T(4,128)} %param.13) | copy-start | bytes 23044
  126.1 8.8 %collective-permute-start.4 = (f32[6,2560]{1,0:T(8,128)S(1)}, f32[6,2560]{1,0:T(8,128)S(1)}, u32[]{:S(2)}, u32[]{:S(2)}) collective-permute-start(f32[6,2560]{1,0:T(8,128)S(1)} %all_gather.13), channel_id=1, source_target_pairs={{0,8},{4,12},{8,16},{12,20},{16,24},{20,28},{1,9},{5,13},{9,17},{1... | collective-permute-start | bytes 184328 | tf_op jit(solution)/shard_map/ppermute | solution.py:17
  127.4 7.6 %collective-permute-start.5 = (f32[6,2560]{1,0:T(8,128)S(1)}, f32[6,2560]{1,0:T(8,128)S(1)}, u32[]{:S(2)}, u32[]{:S(2)}) collective-permute-start(f32[6,2560]{1,0:T(8,128)S(1)} %all_gather.13), channel_id=1, source_target_pairs={{0,4},{4,8},{8,12},{12,16},{16,20},{20,24},{24,28},{1,5},{5,9},{9,... | collective-permute-start | bytes 184328 | tf_op jit(solution)/shard_map/ppermute | solution.py:17
  129.3 7.5 %collective-permute-start.6 = (f32[6,2560]{1,0:T(8,128)S(1)}, f32[6,2560]{1,0:T(8,128)S(1)}, u32[]{:S(2)}, u32[]{:S(2)}) collective-permute-start(f32[6,2560]{1,0:T(8,128)S(1)} %all_gather.13), channel_id=1, source_target_pairs={{4,0},{8,4},{12,8},{16,12},{20,16},{24,20},{28,24},{5,1},{9,5},{13... | collective-permute-start | bytes 184328 | tf_op jit(solution)/shard_map/ppermute | solution.py:17
  133.2 6.3 %collective-permute-start.7 = (f32[6,2560]{1,0:T(8,128)S(1)}, f32[6,2560]{1,0:T(8,128)S(1)}, u32[]{:S(2)}, u32[]{:S(2)}) collective-permute-start(f32[6,2560]{1,0:T(8,128)S(1)} %all_gather.13), channel_id=1, source_target_pairs={{8,0},{12,4},{16,8},{20,12},{24,16},{28,20},{9,1},{13,5},{17,9},{2... | collective-permute-start | bytes 184328 | tf_op jit(solution)/shard_map/ppermute | solution.py:17
  197.9 9.0 %collective-permute-start.8 = (f32[6,2560]{1,0:T(8,128)S(1)}, f32[6,2560]{1,0:T(8,128)S(1)}, u32[]{:S(2)}, u32[]{:S(2)}) collective-permute-start(f32[6,2560]{1,0:T(8,128)S(1)} %all_gather.14), channel_id=1, source_target_pairs={{0,8},{4,12},{8,16},{12,20},{16,24},{20,28},{1,9},{5,13},{9,17},{1... | collective-permute-start | bytes 184328 | tf_op jit(solution)/shard_map/ppermute | solution.py:17
  199.2 7.8 %collective-permute-start.9 = (f32[6,2560]{1,0:T(8,128)S(1)}, f32[6,2560]{1,0:T(8,128)S(1)}, u32[]{:S(2)}, u32[]{:S(2)}) collective-permute-start(f32[6,2560]{1,0:T(8,128)S(1)} %all_gather.14), channel_id=1, source_target_pairs={{0,4},{4,8},{8,12},{12,16},{16,20},{20,24},{24,28},{1,5},{5,9},{9,... | collective-permute-start | bytes 184328 | tf_op jit(solution)/shard_map/ppermute | solution.py:17
  202.6 7.2 %collective-permute-start.10 = (f32[6,2560]{1,0:T(8,128)S(1)}, f32[6,2560]{1,0:T(8,128)S(1)}, u32[]{:S(2)}, u32[]{:S(2)}) collective-permute-start(f32[6,2560]{1,0:T(8,128)S(1)} %all_gather.14), channel_id=1, source_target_pairs={{4,0},{8,4},{12,8},{16,12},{20,16},{24,20},{28,24},{5,1},{9,5},{13... | collective-permute-start | bytes 184328 | tf_op jit(solution)/shard_map/ppermute | solution.py:17
  205.1 6.3 %collective-permute-start.11 = (f32[6,2560]{1,0:T(8,128)S(1)}, f32[6,2560]{1,0:T(8,128)S(1)}, u32[]{:S(2)}, u32[]{:S(2)}) collective-permute-start(f32[6,2560]{1,0:T(8,128)S(1)} %all_gather.14), channel_id=1, source_target_pairs={{8,0},{12,4},{16,8},{20,12},{24,16},{28,20},{9,1},{13,5},{17,9},{2... | collective-permute-start | bytes 184328 | tf_op jit(solution)/shard_map/ppermute | solution.py:17
  266.1 27.8 %copy-start.4 = (f32[3,640]{1,0:T(4,128)}, f32[3,640]{1,0:T(4,128)S(1)}, u32[]{:S(2)}) copy-start(f32[3,640]{1,0:T(4,128)S(1)} %multiply_add_fusion) | copy-start | bytes 23044
  271.4 11.6 %collective-permute-start.12 = (f32[6,2560]{1,0:T(8,128)S(1)}, f32[6,2560]{1,0:T(8,128)S(1)}, u32[]{:S(2)}, u32[]{:S(2)}) collective-permute-start(f32[6,2560]{1,0:T(8,128)S(1)} %all_gather.15), channel_id=1, source_target_pairs={{0,12},{4,16},{8,20},{12,24},{16,28},{1,13},{5,17},{9,21},{13,25},... | collective-permute-start | bytes 184328 | tf_op jit(solution)/shard_map/ppermute | solution.py:17
  272.7 11.9 %collective-permute-start.13 = (f32[6,2560]{1,0:T(8,128)S(1)}, f32[6,2560]{1,0:T(8,128)S(1)}, u32[]{:S(2)}, u32[]{:S(2)}) collective-permute-start(f32[6,2560]{1,0:T(8,128)S(1)} %all_gather.15), channel_id=1, source_target_pairs={{0,8},{4,12},{8,16},{12,20},{16,24},{20,28},{1,9},{5,13},{9,17},{1... | collective-permute-start | bytes 184328 | tf_op jit(solution)/shard_map/ppermute | solution.py:17
  275.7 8.9 %collective-permute-start.14 = (f32[6,2560]{1,0:T(8,128)S(1)}, f32[6,2560]{1,0:T(8,128)S(1)}, u32[]{:S(2)}, u32[]{:S(2)}) collective-permute-start(f32[6,2560]{1,0:T(8,128)S(1)} %all_gather.15), channel_id=1, source_target_pairs={{0,4},{4,8},{8,12},{12,16},{16,20},{20,24},{24,28},{1,5},{5,9},{9,... | collective-permute-start | bytes 184328 | tf_op jit(solution)/shard_map/ppermute | solution.py:17
  279.8 7.6 %collective-permute-start.15 = (f32[6,2560]{1,0:T(8,128)S(1)}, f32[6,2560]{1,0:T(8,128)S(1)}, u32[]{:S(2)}, u32[]{:S(2)}) collective-permute-start(f32[6,2560]{1,0:T(8,128)S(1)} %all_gather.15), channel_id=1, source_target_pairs={{4,0},{8,4},{12,8},{16,12},{20,16},{24,20},{28,24},{5,1},{9,5},{13... | collective-permute-start | bytes 184328 | tf_op jit(solution)/shard_map/ppermute | solution.py:17
  281.7 6.7 %collective-permute-start.16 = (f32[6,2560]{1,0:T(8,128)S(1)}, f32[6,2560]{1,0:T(8,128)S(1)}, u32[]{:S(2)}, u32[]{:S(2)}) collective-permute-start(f32[6,2560]{1,0:T(8,128)S(1)} %all_gather.15), channel_id=1, source_target_pairs={{8,0},{12,4},{16,8},{20,12},{24,16},{28,20},{9,1},{13,5},{17,9},{2... | collective-permute-start | bytes 184328 | tf_op jit(solution)/shard_map/ppermute | solution.py:17
  283.1 54.9 %copy-start.5 = (f32[3,4]{1,0:T(4,128)}, f32[3,4]{1,0:T(4,128)S(1)}, u32[]{:S(2)}) copy-start(f32[3,4]{1,0:T(4,128)S(1)} %multiply_add_fusion.7) | copy-start | bytes 148
  283.1 10.8 %collective-permute-start.17 = (f32[6,2560]{1,0:T(8,128)S(1)}, f32[6,2560]{1,0:T(8,128)S(1)}, u32[]{:S(2)}, u32[]{:S(2)}) collective-permute-start(f32[6,2560]{1,0:T(8,128)S(1)} %all_gather.15), channel_id=1, source_target_pairs={{12,0},{16,4},{20,8},{24,12},{28,16},{13,1},{17,5},{21,9},{25,13},... | collective-permute-start | bytes 184328 | tf_op jit(solution)/shard_map/ppermute | solution.py:17
  293.9 0.7 copy-start.2
  293.9 0.7 copy-start.3
